TPU v7x, 32 devices: a whole 2x2x4 slice. The times are simulated.
32 devices in a mesh: dp: 1, tp: 32 (over x, y, z, core).
Axes of the slice: x: 2, y: 2, z: 4, core: 2. Of those that a mesh axis runs over, the one named last changes fastest.
Arguments:
- x: bfloat16 [2048, 12288], P('dp')
- w_gate: bfloat16 [12288, 28672], P(None, 'tp')
- w_up: bfloat16 [12288, 28672], P(None, 'tp')
- w_down: bfloat16 [28672, 12288], P('tp')
Outputs:
- output: bfloat16 [2048, 12288], P('dp')
All inputs are finite; a program needn't handle non-finite values.
Results may differ from a plain program's by a relative error of at most 0.016.
Values are sent between devices in bfloat16 or wider.
A program may use at most 2 GiB of HBM per device.

v0:
```python
import jax
import jax.numpy as jnp
from jax import lax
from jax.sharding import PartitionSpec as P


def solution(mesh):
    def step(x, w_gate, w_up, w_down):
        gate = jnp.dot(x, w_gate, preferred_element_type=jnp.float32)
        up = jnp.dot(x, w_up, preferred_element_type=jnp.float32)
        hidden = (jax.nn.silu(gate) * up).astype(jnp.bfloat16)
        term = jnp.dot(hidden, w_down, preferred_element_type=jnp.float32).astype(jnp.bfloat16)
        return lax.psum(term, "tp")

    return jax.shard_map(
        step,
        mesh=mesh,
        in_specs=(P("dp", None), P(None, "tp"), P(None, "tp"), P("tp", None)),
        out_specs=P("dp", None),
        check_vma=False,
    )
```

profile of v0, /device:TPU:0, one launch (start us, length us, event | category | flops | bytes accessed | tf_op | source)
XLA Modules:
  0.0 959.7 jit_solution(2527828040972195514)
XLA Ops:
  6.5 0.0 all-reduce.2.cloned.1.call-start
  6.5 59.4 %fusion = f32[2048,896]{1,0:T(8,128)S(1)} fusion(bf16[2048,12288]{1,0:T(8,128)(2,1)} %param.4, bf16[12288,896]{1,0:T(8,128)(2,1)} %param.5), kind=kOutput, calls=%fused_computation.2 | convolution fusion | flops 45097156608 | bytes 79691776 | tf_op jit(solution)/shard_map/dot_general | solution.py:9
  66.0 63.4 %multiply_convert_fusion = bf16[2048,896]{1,0:T(8,128)(2,1)S(1)} fusion(f32[2048,896]{1,0:T(8,128)S(1)} %fusion, bf16[2048,12288]{1,0:T(8,128)(2,1)} %param.4, bf16[12288,896]{1,0:T(8,128)(2,1)} %param.6), kind=kOutput, calls=%fused_computation.1 | convolution fusion | flops 45108166656 | bytes 83361792 | tf_op jit(solution)/shard_map/dot_general | solution.py:10
  129.3 65.4 %convolution_convert_fusion = bf16[2048,12288]{1,0:T(8,128)(2,1)} fusion(bf16[2048,896]{1,0:T(8,128)(2,1)S(1)} %multiply_convert_fusion, bf16[896,12288]{1,0:T(8,128)(2,1)} %param.7), kind=kOutput, calls=%fused_computation | convolution fusion | flops 45122322432 | bytes 76021760 | tf_op jit(solution)/shard_map/dot_general | solution.py:12
  194.7 0.0 all-reduce.2.cloned.1.call-update
  194.7 724.4 %all-reduce.2.cloned.1.call-done = bf16[2048,12288]{1,0:T(8,128)(2,1)} async-done(((bf16[2048,12288]{1,0:T(8,128)(2,1)}), bf16[2048,12288]{1,0:T(8,128)(2,1)}) %all-reduce.2.cloned.1.call-update) | async-done | bytes 50331664 | tf_op jit(solution)/shard_map/psum | solution.py:13
  919.1 33.7 %copy.6 = bf16[2048,12288]{1,0:T(8,128)(2,1)} copy(bf16[2048,12288]{1,0:T(8,128)(2,1)} %all-reduce.2.cloned.1.call-done) | data formatting | bytes 100663296
Async XLA Ops:
  6.5 912.5 %all-reduce.2.cloned.1.call-start = ((), (), s32[]{:S(2)}) async-start(), calls=%async_computation | async-start | bytes 100663296 | tf_op jit(solution)/shard_map/psum | solution.py:13
Sparse Core Ops, SparseCore 0:
  194.8 724.1 all-reduce.1
where the time goes:
time: 960 us
  waiting for transfers between devices  724 us (75%)
  matrix products  188 us (20%)
  local copies, waits for them, and re-layouts  33.7 us (4%)
  between operations  13.4 us (1%)
    psum x1, waiting for transfers between devices, step(): return lax.psum(term, 'tp')  724 us
    dot_general x1, matrix products, step(): jnp.dot(hidden, w_down, preferred_element_type=jnp.float32)  65.4 us
    dot_general x1, matrix products, step(): up = jnp.dot(x, w_up, preferred_element_type=jnp.float32)  63.4 us
    dot_general x1, matrix products, step(): gate = jnp.dot(x, w_gate, preferred_element_type=jnp.float32)  59.4 us
    unnamed x1, local copies, waits for them, and re-layouts  33.7 us
  transfers between devices with their start and end apart: 1, of which 1 were waited for; matrix products, arithmetic and copies ran while one was open for 0% of the time, Pallas kernels for 0%

commit v1 on v0

v1 whole, which is shorter than its diff:
```python
import functools

import jax
import jax.numpy as jnp
from jax import lax
from jax.experimental import pallas as pl
from jax.experimental.pallas import tpu as pltpu
from jax.sharding import PartitionSpec as P

F32 = jnp.float32
BF16 = jnp.bfloat16
MESH = pl.DeviceIdType.MESH


def dims(rows, d, ff, chunk, pieces):
    wa = d // 24
    return dict(n=rows // chunk, R=chunk, D=d, FF=ff, WA=wa, H=wa // 2, WB=wa // 4, NK=pieces, KB=d // pieces)


def body(cfg, x_ref, wg_ref, wu_ref, wdh_ref, ta, tb, wd, h, xb, wgb, wub, accg, accu, ps, pr, a2s, a2r, a3s, a3r, t1s, t1r, t2s, t2r,
         b1s, b1r, b2s, b2r, b3s, b3r, b4s, b4r, b5s, b5r, fa, fb,
         wd_m, g_m, p_s, p_m, a2_s, a2_m, a3_s, a3_m, t1_s, t1_m, t2_s, t2_m, b1_s, b1_m, b2_s, b2_m, b3_s, b3_m, b4_s, b4_m, b5_s, b5_m,
         la_m, lb_m, fa_s, fb_s, q_s, g1_m, g2_m, g3_m, g4_m, g5_m, h1_m, h2_m, hz_m, h5_m,
         cp, ca2, ca3, ct1, ct2, cb1, cb2, cb3, cb4, cb5):
    n, R, D, WA, H, WB, NK, KB = (cfg[k] for k in ("n", "R", "D", "WA", "H", "WB", "NK", "KB"))
    NB = xb.shape[0]
    me = lax.axis_index("tp")
    dp = lax.axis_index("dp")
    x, y, z, c = me // 16, (me // 8) % 2, (me // 2) % 4, me % 2

    def dev(x, y, z, c):
        return (dp, ((x * 2 + y) * 4 + z) * 2 + c)

    outer = (z == 0) | (z == 3)
    inner = jnp.logical_not(outer)
    up_ok, dn_ok = z < 3, z > 0
    zu, zd = jnp.minimum(z + 1, 3), jnp.maximum(z - 1, 0)
    zin = jnp.where(outer, jnp.where(z == 0, 1, 2), 3 - z)
    zout = jnp.where(z < 2, 0, 3)
    near = jnp.where(z < 2, 0, 1)
    far = 1 - near
    partner = dev(x, y, z, 1 - c)
    xn, yn = dev(1 - x, y, z, c), dev(x, 1 - y, z, c)
    up, down, zin_d, zout_d = dev(x, y, zu, c), dev(x, y, zd, c), dev(x, y, zin, c), dev(x, y, zout, c)
    go, gx, gy, gd = x * 2 + y, (1 - x) * 2 + y, x * 2 + 1 - y, (1 - x) * 2 + 1 - y

    def pick(order, a, b):
        first = order == 0
        return jax.tree.map(lambda p, q: jnp.where(first, p, q), a, b)

    def fn(order):
        return pick(order, xn, yn)

    def sn(order):
        return pick(order, yn, xn)

    def gf(order):
        return pick(order, gx, gy)

    def gs(order):
        return pick(order, gy, gx)

    def copy(src, dst, ss, rs, to):
        return pltpu.make_async_remote_copy(src, dst, ss, rs, device_id=to, device_id_type=MESH)

    def signal(sem, to):
        pl.semaphore_signal(sem, inc=1, device_id=to, device_id_type=MESH)

    def col_a(core, order, g, half=0):
        return core * (8 * WA) + order * (4 * WA) + g * WA + half * H

    def col_b(core, q, g=0):
        return 16 * WA + core * (16 * WB) + q * (4 * WB) + g * WB

    def lanes(i, w):
        return pl.ds(pl.multiple_of(i * w, w), w)

    def dot(i, col, w, unit):
        return jnp.dot(h[i % 3], wd[:, pl.ds(pl.multiple_of(col, unit), w)], preferred_element_type=F32)

    def c_p(s):
        return copy(ps, pr.at[s], p_s, p_m.at[s], partner)

    def c_a2(s, o, m):
        return copy(a2s.at[o, m], a2r.at[s, o, m], a2_s.at[o, m], a2_m.at[s, o, m], fn(o))

    def c_a3(s, o):
        return copy(a3s.at[o], a3r.at[s, o], a3_s.at[o], a3_m.at[s, o], sn(o))

    def c_t1(o):
        return copy(t1s.at[o], t1r.at[o], t1_s.at[o], t1_m.at[o], zin_d)

    def c_t2(src, o):
        return copy(t2s.at[o], t2r.at[src, o], t2_s.at[o], t2_m.at[src, o], zin_d)

    def c_b1():
        return copy(b1s, b1r, b1_s, b1_m, zin_d)

    def c_b2(d):
        return copy(b2s, b2r.at[d], b2_s, b2_m.at[d], zin_d)

    def c_b3(d, to=up):
        return copy(b3s.at[d], b3r.at[d], b3_s.at[d], b3_m.at[d], to)

    def c_b4(o, m):
        return copy(b4s.at[m], b4r.at[m], b4_s.at[m], b4_m.at[m], fn(o))

    def c_b5(o):
        return copy(b5s, b5r, b5_s, b5_m, sn(o))

    def g_copies(kk):
        i, k, b = kk // NK, kk % NK, kk % NB
        rows, ks = pl.ds(pl.multiple_of(i * R, R), R), pl.ds(pl.multiple_of(k * KB, KB), KB)
        return (pltpu.make_async_copy(x_ref.at[rows, ks], xb.at[b], g_m.at[b, 0]),
                pltpu.make_async_copy(wg_ref.at[ks], wgb.at[b], g_m.at[b, 1]),
                pltpu.make_async_copy(wu_ref.at[ks], wub.at[b], g_m.at[b, 2]))

    def g_pieces(i, k0, k1):
        def step(k, _):
            kk = i * NK + k
            b = kk % NB
            for cp_ in g_copies(kk):
                cp_.wait()

            @pl.when(kk + NB - 1 < n * NK)
            def _():
                for cp_ in g_copies(kk + NB - 1):
                    cp_.start()

            @pl.when(k == 0)
            def _():
                accg[...] = jnp.zeros_like(accg)
                accu[...] = jnp.zeros_like(accu)

            accg[...] += jnp.dot(xb[b], wgb[b], preferred_element_type=F32)
            accu[...] += jnp.dot(xb[b], wub[b], preferred_element_type=F32)
            return 0

        lax.fori_loop(k0, k1, step, 0)
        if k1 == NK:
            h[i % 3] = (jax.nn.silu(accg[...]) * accu[...]).astype(BF16)

    def s1(t):
        @pl.when(t >= 1)
        def _():
            c_p(0).wait_send()

        @pl.when(t >= 2)
        def _():
            pl.semaphore_wait(cp, 1)

        def step(j, _):
            col = jnp.where(j < 8, col_a(1 - c, 0, j), col_b(1 - c, j - 8))
            ps[j] = dot(t, col, WA, WA).astype(BF16)
            copy(ps.at[j], pr.at[t % 2, j], p_s, p_m.at[t % 2], partner).start()
            return 0

        lax.fori_loop(0, 12, step, 0)

    def s2(t, m):
        def step(o, _):
            @pl.when(t >= 1)
            def _():
                c_a2(0, o, m).wait_send()

            if m == 0:
                @pl.when(t >= 2)
                def _():
                    pl.semaphore_wait(ca2.at[o], 1)

            g = gf(o) if m else gd
            v = dot(t, col_a(c, o, g), WA, WA) + pr[t % 2, o * 4 + g].astype(F32)
            a2s[o, m] = v.astype(BF16)
            c_a2(t % 2, o, m).start()
            return 0

        lax.fori_loop(0, 2, step, 0)

    def s3(t):
        def step(o, _):
            @pl.when(t >= 1)
            def _():
                c_a3(0, o).wait_send()

            @pl.when(t >= 2)
            def _():
                pl.semaphore_wait(ca3.at[o], 1)

            c_a2(t % 2, o, 0).wait_recv()
            g = gs(o)
            v = dot(t, col_a(c, o, g), WA, WA) + pr[t % 2, o * 4 + g].astype(F32) + a2r[t % 2, o, 0].astype(F32)
            a3s[o] = v.astype(BF16)
            c_a3(t % 2, o).start()
            return 0

        lax.fori_loop(0, 2, step, 0)

    def t1(t):
        c_p(t % 2).wait_recv()

        @pl.when(outer)
        def _():
            @pl.when(t >= 1)
            def _():
                c_b1().wait_send()
                pl.semaphore_wait(cb1, 1)

            q = 3 - z
            b1s[...] = (dot(t, col_b(c, q), WA, WA) + pr[t % 2, 8 + q].astype(F32)).astype(BF16)
            c_b1().start()

    def t2(t):
        @pl.when(t >= 1)
        def _():
            c_b2(0).wait_send()
            pl.semaphore_wait(cb2, 1)

        @pl.when(inner)
        def _():
            c_b1().wait_recv()

        q = (z + 2) % 4
        b2s[...] = (dot(t, col_b(c, q), WA, WA) + pr[t % 2, 8 + q].astype(F32) + b1r[...].astype(F32)).astype(BF16)
        d = jnp.where(z < 2, 0, 1)
        c_b2(d).start()

        @pl.when(inner & (t + 1 < n))
        def _():
            signal(cb1, zout_d)

    def s4(u):
        for o in range(2):
            c_a3(u % 2, o).wait_recv()
            c_a2(u % 2, o, 1).wait_recv()

        @pl.when(outer)
        def _():
            def step(o, _):
                @pl.when(u >= 1)
                def _():
                    c_t1(o).wait_send()

                @pl.when((u >= 1) & (o == 0))
                def _():
                    pl.semaphore_wait(ct1, 1)

                t1s[o] = own_a(u, o, far).astype(BF16)
                c_t1(o).start()
                return 0

            lax.fori_loop(0, 2, step, 0)

    def own_a(u, o, half):
        s, ln = u % 2, lanes(half, H)
        return (dot(u, col_a(c, o, go, half), H, H) + pr[s, o * 4 + go, :, ln].astype(F32)
                + a2r[s, o, 1, :, ln].astype(F32) + a3r[s, o, :, ln].astype(F32))

    def s5(u):
        src = jnp.where(outer, 0, 1)

        def step(o, _):
            @pl.when(u >= 1)
            def _():
                c_t2(src, o).wait_send()

            @pl.when((u >= 1) & (o == 0))
            def _():
                pl.semaphore_wait(ct2, 1)

            @pl.when(inner)
            def _():
                c_t1(o).wait_recv()

            half = jnp.where(outer, near, far)
            t2s[o] = (own_a(u, o, half) + t1r[o].astype(F32)).astype(BF16)
            c_t2(src, o).start()
            return 0

        lax.fori_loop(0, 2, step, 0)

        @pl.when(inner & (u + 1 < n))
        def _():
            signal(ct1, zout_d)

    def win_a(u, o, g, half):
        return ta.at[u, c, o, g, half]

    def fa_copies(u, o):
        w = win_a(u, o, go, near)
        f = fa.at[o]
        return ((f, w, fa_s.at[o, 0], g1_m.at[u], zout_d), (f, w, fa_s.at[o, 1], g1_m.at[u], zin_d),
                (f, w, fa_s.at[o, 2], g3_m.at[0, u], sn(o)), (f, w, fa_s.at[o, 3], g4_m.at[0, u], fn(o)),
                (f, w, fa_s.at[o, 4], g5_m.at[u], partner))

    def fa_done(u, o):
        for a in fa_copies(u, o):
            copy(*a).wait_send()
        pltpu.make_async_copy(fa.at[o], win_a(u, o, go, near), la_m.at[o]).wait()

    def s6(u):
        @pl.when(inner)
        def _():
            for o in range(2):
                for src in range(2):
                    c_t2(src, o).wait_recv()

            def step(o, _):
                @pl.when(u >= 1)
                def _():
                    fa_done(u, o)

                fa[o] = (own_a(u, o, near) + t2r[0, o].astype(F32) + t2r[1, o].astype(F32)).astype(BF16)
                pltpu.make_async_copy(fa.at[o], win_a(u, o, go, near), la_m.at[o]).start()
                for a in fa_copies(u, o):
                    copy(*a).start()
                return 0

            lax.fori_loop(0, 2, step, 0)

            @pl.when(u + 1 < n)
            def _():
                signal(ct2, zout_d)
                signal(ct2, zin_d)

        @pl.when(u + 2 < n)
        def _():
            for o in range(2):
                signal(ca2.at[o], fn(o))
                signal(ca3.at[o], sn(o))

    def t3(u):
        def step(d, _):
            ok = jnp.where(d == 0, up_ok, dn_ok)

            @pl.when(ok)
            def _():
                to = pick(d, up, down)

                @pl.when(u >= 1)
                def _():
                    c_b3(d, to).wait_send()
                    pl.semaphore_wait(cb3.at[d], 1)

                @pl.when(inner)
                def _():
                    c_b2(d).wait_recv()

                q = pick(d, zu, zd)
                b3s[d] = (dot(u, col_b(c, q), WA, WA) + pr[u % 2, 8 + q].astype(F32) + b2r[d].astype(F32)).astype(BF16)
                c_b3(d, to).start()

            return 0

        lax.fori_loop(0, 2, step, 0)

        @pl.when(inner & (u + 1 < n))
        def _():
            signal(cb2, zout_d)
            signal(cb2, zin_d)

    def own_b(u, g):
        ln = lanes(g, WB)
        return (dot(u, col_b(c, z, g), WB, WB) + pr[u % 2, 8 + z, :, ln].astype(F32)
                + b3r[0, :, ln].astype(F32) + b3r[1, :, ln].astype(F32))

    def t4(u):
        @pl.when(dn_ok)
        def _():
            c_b3(0).wait_recv()

        @pl.when(up_ok)
        def _():
            c_b3(1).wait_recv()

        o = u % 2

        def step(m, _):
            @pl.when(u >= 1)
            def _():
                c_b4(o, m).wait_send()

            @pl.when((u >= 1) & (m == 0))
            def _():
                pl.semaphore_wait(cb4, 1)

            b4s[m] = own_b(u, jnp.where(m == 0, gd, gf(o))).astype(BF16)
            c_b4(o, m).start()
            return 0

        lax.fori_loop(0, 2, step, 0)

    def t5(u):
        o = u % 2

        @pl.when(u >= 1)
        def _():
            c_b5(o).wait_send()
            pl.semaphore_wait(cb5, 1)

        c_b4(o, 0).wait_recv()
        b5s[...] = (own_b(u, gs(o)) + b4r[0].astype(F32)).astype(BF16)
        c_b5(o).start()

    def fb_copies(u):
        w, o = tb.at[u, c, z, go], u % 2
        return ((fb, w, fb_s.at[0], h1_m.at[u], sn(o)), (fb, w, fb_s.at[1], h2_m.at[0, u], fn(o)))

    def fb_local(u):
        return pltpu.make_async_copy(fb, tb.at[u, c, z, go], lb_m)

    def t6(u):
        o = u % 2
        c_b4(o, 1).wait_recv()
        c_b5(o).wait_recv()

        @pl.when(u >= 1)
        def _():
            for a in fb_copies(u):
                copy(*a).wait_send()

        fb[...] = (own_b(u, go) + b4r[1].astype(F32) + b5r[...].astype(F32)).astype(BF16)
        fb_local(u).start()
        for a in fb_copies(u):
            copy(*a).start()

        @pl.when(u + 1 < n)
        def _():
            @pl.when(dn_ok)
            def _():
                signal(cb3.at[0], down)

            @pl.when(up_ok)
            def _():
                signal(cb3.at[1], up)

            signal(cb4, fn(1 - o))
            signal(cb5, sn(1 - o))

        @pl.when(u + 2 < n)
        def _():
            signal(cp, partner)

    def go_on(v, cond, k, src, rs, to):
        def make():
            return copy(src(v), src(v), q_s.at[k], rs(v), to)

        @pl.when(cond if cond is not True else v >= 0)
        def _():
            @pl.when(v >= 1)
            def _():
                make().wait_send()

            make().start()

    plan = []

    def op(group, cond, src, rs, to):
        plan.append((group, cond, len(plan), src, rs, to))

    def half_ops(group, cond, half, which):
        for o in range(2):
            w = functools.partial(lambda o, half, v: win_a(v, o, go, half), o, half)
            op(group, cond, w, functools.partial(lambda k, v: g3_m.at[k, v], which), sn(o))
            op(group, cond, w, functools.partial(lambda k, v: g4_m.at[k, v], which), fn(o))
            op(group, cond, w, lambda v: g5_m.at[v], partner)

    for o in range(2):
        op("q0", inner, functools.partial(lambda o, v: win_a(v, o, go, far), o), lambda v: g2_m.at[v], zout_d)
    half_ops("q0i", inner, far, 1)
    half_ops("q0o", outer, near, 0)
    half_ops("q1", outer, far, 1)
    for k, half in ((0, near), (1, far)):
        for o in range(2):
            w = functools.partial(lambda o, half, v: win_a(v, o, gs(o), half), o, half)
            op(f"q{2 + k}", True, w, functools.partial(lambda k, v: g4_m.at[2 + k, v], k), fn(o))
            op(f"q{2 + k}", True, w, lambda v: g5_m.at[v], partner)
    for o in range(2):
        for half in range(2):
            op("q4", True, functools.partial(lambda o, half, v: win_a(v, o, gf(o), half), o, half), lambda v: g5_m.at[v], partner)
            op("q5", True, functools.partial(lambda o, half, v: win_a(v, o, gd, half), o, half), lambda v: g5_m.at[v], partner)
    op("r0", True, lambda v: tb.at[v, c, z, gs(v % 2)], lambda v: h2_m.at[1, v], None)
    block = lambda q: (lambda v: tb.at[v, c, q])
    op("r1", up_ok, block(z), lambda v: hz_m.at[0, v], up)
    op("r1", dn_ok, block(z), lambda v: hz_m.at[1, v], down)
    op("r1", True, block(z), lambda v: h5_m.at[v], partner)
    zm2, zp2 = jnp.maximum(z - 2, 0), jnp.minimum(z + 2, 3)
    op("r2u", dn_ok & up_ok, block(zd), lambda v: hz_m.at[2, v], up)
    op("r2u", dn_ok, block(zd), lambda v: h5_m.at[v], partner)
    op("r2d", dn_ok & up_ok, block(zu), lambda v: hz_m.at[3, v], down)
    op("r2d", up_ok, block(zu), lambda v: h5_m.at[v], partner)
    op("r3u", z == 2, block(zm2), lambda v: hz_m.at[4, v], up)
    op("r3u", z >= 2, block(zm2), lambda v: h5_m.at[v], partner)
    op("r3d", z == 1, block(zp2), lambda v: hz_m.at[5, v], down)
    op("r3d", z <= 1, block(zp2), lambda v: h5_m.at[v], partner)
    op("r4", outer, block(3 - z), lambda v: h5_m.at[v], partner)

    def run(group, v):
        for g_, cond, k, src, rs, to in plan:
            if g_ == group:
                go_on(v, cond, k, src, rs, fn(v % 2) if to is None else to)

    def arrived(ref, sem):
        copy(ref, ref, q_s.at[0], sem, partner).wait_recv()

    def pair(v):
        return ta.at[v, c, :, 0, 0]

    def q0a(v):
        arrived(pair(v), g1_m.at[v])
        run("q0", v)
        run("q0i", v)
        run("q0o", v)

    def q0b(v):
        arrived(tb.at[v, c, 0, 0], h1_m.at[v])
        run("r0", v)

    def q1a(v):
        @pl.when(outer)
        def _():
            arrived(pair(v), g2_m.at[v])

        run("q1", v)

    def q1b(v):
        fb_local(v).wait()
        for k in range(2):
            arrived(tb.at[v, c, 0, 0], h2_m.at[k, v])
        run("r1", v)

    def q2a(v):
        arrived(pair(v), g3_m.at[0, v])
        run("q2", v)

    def q3a(v):
        arrived(pair(v), g3_m.at[1, v])
        run("q3", v)

    def hop(v, up_there, down_there, k, groups):
        for there, kk, g in ((up_there, k, groups[0]), (down_there, k + 1, groups[1])):
            @pl.when(there)
            def _():
                arrived(tb.at[v, c, 0], hz_m.at[kk, v])

            run(g, v)

    def q2b(v):
        hop(v, dn_ok, up_ok, 0, ("r2u", "r2d"))

    def q3b(v):
        hop(v, z >= 2, z <= 1, 2, ("r3u", "r3d"))

    def q4b(v):
        hop(v, z == 3, z == 0, 4, ("", "r4"))

    def q4a(v):
        for k in range(2):
            arrived(pair(v), g4_m.at[k, v])
        run("q4", v)

    def q5(v):
        for k in range(2):
            arrived(pair(v), g4_m.at[2 + k, v])
        run("q5", v)

    @pl.when(outer)
    def _():
        t1r[...] = jnp.zeros_like(t1r)
        b1r[...] = jnp.zeros_like(b1r)
        b2r[...] = jnp.zeros_like(b2r)

    @pl.when(z == 0)
    def _():
        b3r[0] = jnp.zeros_like(b3r[0])

    @pl.when(z == 3)
    def _():
        b3r[1] = jnp.zeros_like(b3r[1])

    for kk in range(NB - 1):
        for cp_ in g_copies(kk):
            cp_.start()

    def wd_copies():
        out = []
        for k, core in enumerate((1 - c, c)):
            for m, (off, w) in enumerate(((col_a(core, 0, 0), 8 * WA), (col_b(core, 0), 16 * WB))):
                cols = pl.ds(pl.multiple_of(off, w), w)
                out.append(pltpu.make_async_copy(wdh_ref.at[:, cols], wd.at[:, cols], wd_m.at[2 * k + m]))
        return out

    g_pieces(0, 0, NK // 2)
    for cp_ in wd_copies():
        cp_.start()
    g_pieces(0, NK // 2, NK)
    cut = [NK * k // 8 for k in range(9)]

    def slot(t, _):
        @pl.when(t == 0)
        def _():
            for cp_ in wd_copies():
                cp_.wait()

        def at(i, f):
            @pl.when((i >= 0) & (i < n))
            def _():
                f(i)

        def g(a, b):
            at(t + 1, lambda i: g_pieces(i, cut[a], cut[b]))

        u, v, w, e = t - 1, t - 2, t - 3, t - 4
        at(u, t3)
        at(t, s1)
        at(w, q2b)
        at(v, q0a)
        at(u, s4)
        g(0, 1)
        at(t, t1)
        at(v, q0b)
        at(u, t4)
        at(t, lambda i: s2(i, 0))
        g(1, 2)
        at(e, q2a)
        at(u, s5)
        at(w, q3a)
        at(w, q3b)
        g(2, 3)
        at(u, t5)
        g(3, 4)
        at(t, lambda i: s2(i, 1))
        at(t, t2)
        at(v, q1b)
        g(4, 5)
        at(t, s3)
        g(5, 7)
        at(u, s6)
        at(u, t6)
        at(e, q4a)
        at(e, q5)
        at(v, q1a)
        g(7, 8)
        at(e, q4b)
        return 0

    lax.fori_loop(0, n + 4, slot, 0)

    last = n - 1
    c_p(0).wait_send()
    for o in range(2):
        for m in range(2):
            c_a2(0, o, m).wait_send()
        c_b4(0, o).wait_send()
        c_a3(0, o).wait_send()
        c_t2(0, o).wait_send()

        @pl.when(outer)
        def _():
            c_t1(o).wait_send()

        @pl.when(inner)
        def _():
            fa_done(last, o)

        @pl.when(up_ok if o == 0 else dn_ok)
        def _():
            c_b3(o).wait_send()

    @pl.when(outer)
    def _():
        c_b1().wait_send()

    c_b2(0).wait_send()
    c_b5(0).wait_send()
    for a in fb_copies(last):
        copy(*a).wait_send()
    for g_, cond, k, src, rs, to in plan:
        def done(k=k, src=src, rs=rs):
            copy(src(last), src(last), q_s.at[k], rs(last), partner).wait_send()

        if cond is True:
            done()
        else:
            pl.when(cond)(done)

    def all_here(v, _):
        arrived(ta.at[v, 1 - c], g5_m.at[v])
        arrived(tb.at[v, 1 - c], h5_m.at[v])
        return 0

    lax.fori_loop(0, n, all_here, 0)


N_OPS = 2 + 6 * 3 + 8 + 8 + 1 + 3 + 8 + 1


def block_sums(cfg, x, w_gate, w_up, w_down):
    n, R, D, FF, WA, H, WB, KB = (cfg[k] for k in ("n", "R", "D", "FF", "WA", "H", "WB", "KB"))
    NB = 4
    vm = lambda *s: pltpu.VMEM(s, BF16)
    dma = lambda *s: pltpu.SemaphoreType.DMA(s) if s else pltpu.SemaphoreType.DMA
    reg = lambda *s: pltpu.SemaphoreType.REGULAR(s) if s else pltpu.SemaphoreType.REGULAR
    scratch = [
        vm(FF, D), vm(3, R, FF), vm(NB, R, KB), vm(NB, KB, FF), vm(NB, KB, FF), pltpu.VMEM((R, FF), F32), pltpu.VMEM((R, FF), F32),
        vm(12, R, WA), vm(2, 12, R, WA), vm(2, 2, R, WA), vm(2, 2, 2, R, WA), vm(2, R, WA), vm(2, 2, R, WA),
        vm(2, R, H), vm(2, R, H), vm(2, R, H), vm(2, 2, R, H),
        vm(R, WA), vm(R, WA), vm(R, WA), vm(2, R, WA), vm(2, R, WA), vm(2, R, WA), vm(2, R, WB), vm(2, R, WB), vm(R, WB), vm(R, WB),
        vm(2, R, H), vm(R, WB),
        dma(4), dma(NB, 3), dma(), dma(2), dma(2, 2), dma(2, 2, 2), dma(2), dma(2, 2), dma(2), dma(2), dma(2), dma(2, 2),
        dma(), dma(), dma(), dma(2), dma(2), dma(2), dma(2), dma(2), dma(), dma(),
        dma(2), dma(), dma(2, 5), dma(2), dma(N_OPS), dma(n), dma(n), dma(2, n), dma(4, n), dma(n), dma(n), dma(2, n), dma(6, n), dma(n),
        reg(), reg(2), reg(2), reg(), reg(), reg(), reg(), reg(2), reg(), reg(),
    ]
    hbm = pl.BlockSpec(memory_space=pl.ANY)
    return pl.pallas_call(
        functools.partial(body, cfg),
        name="mlp_sums",
        out_shape=(jax.ShapeDtypeStruct((n, 2, 2, 4, 2, R, H), BF16), jax.ShapeDtypeStruct((n, 2, 4, 4, R, WB), BF16)),
        in_specs=[hbm] * 4,
        out_specs=(hbm, hbm),
        scratch_shapes=scratch,
        compiler_params=pltpu.CompilerParams(has_side_effects=True, vmem_limit_bytes=66_000_000),
    )(x, w_gate, w_up, w_down)


def place(cfg, ta, tb):
    n, R, D, WA, H, WB = (cfg[k] for k in ("n", "R", "D", "WA", "H", "WB"))
    W, NBUF = 8 * WA, 4

    def kernel(a_ref, b_ref, o_ref, buf, in_m, out_m):
        def ins(i, part, b):
            if part < 2:
                return [pltpu.make_async_copy(a_ref.at[i, part, o, g, k], buf.at[b, :, pl.ds((o * 4 + g) * WA + k * H, H)], in_m.at[b])
                        for o in range(2) for g in range(4) for k in range(2)]
            return [pltpu.make_async_copy(b_ref.at[i, c, q, g], buf.at[b, :, pl.ds(((c * 4 + q) * 4 + g) * WB, WB)], in_m.at[b])
                    for c in range(2) for q in range(4) for g in range(4)]

        def out(s, b):
            i, part = s // 3, s % 3
            rows = pl.ds(pl.multiple_of(i * R, R), R)
            return pltpu.make_async_copy(buf.at[b], o_ref.at[rows, pl.ds(pl.multiple_of(part * W, W), W)], out_m.at[b])

        def start(s):
            b = s % NBUF
            for part in range(3):
                @pl.when(s % 3 == part)
                def _():
                    for cp in ins(s // 3, part, b):
                        cp.start()

        for s in range(2):
            start(s)

        def step(s, _):
            @pl.when(s >= 2)
            def _():
                out(s - 2, (s - 2) % NBUF).wait()

            @pl.when(s + 2 < 3 * n)
            def _():
                start(s + 2)

            b = s % NBUF
            pltpu.make_async_copy(buf.at[b], buf.at[b], in_m.at[b]).wait()
            out(s, b).start()
            return 0

        lax.fori_loop(0, 3 * n, step, 0)
        for s in (3 * n - 2, 3 * n - 1):
            out(s, s % NBUF).wait()

    hbm = pl.BlockSpec(memory_space=pl.ANY)
    return pl.pallas_call(
        kernel,
        name="place",
        out_shape=jax.ShapeDtypeStruct((n * R, D), BF16),
        in_specs=[hbm, hbm],
        out_specs=hbm,
        scratch_shapes=[pltpu.VMEM((NBUF, R, W), BF16), pltpu.SemaphoreType.DMA((NBUF,)), pltpu.SemaphoreType.DMA((NBUF,))],
    )(ta, tb)


def build(mesh, chunk, pieces):
    def step(x, w_gate, w_up, w_down):
        cfg = dims(x.shape[0], x.shape[1], w_gate.shape[1], chunk, pieces)
        return place(cfg, *block_sums(cfg, x, w_gate, w_up, w_down))

    return jax.shard_map(
        step,
        mesh=mesh,
        in_specs=(P("dp", None), P(None, "tp"), P(None, "tp"), P("tp", None)),
        out_specs=P("dp", None),
        check_vma=False,
    )


def solution(mesh):
    return build(mesh, 256, 16)
```

time: 960 us -> 410 us (0.43)
  waiting for transfers between devices: 724 us -> 0 us
  Pallas kernels: 0 us -> 410 us
  matrix products: 188 us -> 0 us
  local copies, waits for them, and re-layouts: 33.7 us -> 0 us
  between operations: 13.4 us -> 0.01 us
    psum x1 -> x0, waiting for transfers between devices: 724 us -> none  [step(): return lax.psum(term, 'tp')]
    pallas_call x0 -> x2, Pallas kernels: none -> 410 us  [the longest x1 376 us: block_sums(): pl.pallas_call(functools.partial(body, cfg), name='mlp_sums', out_shape=(...]
    dot_general x3 -> x0, matrix products: 188 us -> none  [the longest x1 65.4 us: step(): jnp.dot(hidden, w_down, preferred_element_type=jnp.float32)]
    unnamed x1 -> x0, local copies, waits for them, and re-layouts: 33.7 us -> none
  transfers between devices with their start and end apart: 1 -> 0, of which waited for: 1 -> 0; matrix products, arithmetic and copies ran while one was open for 0% -> 0% of each run, Pallas kernels for 0% -> 0%
where the time goes in v1:
time: 410 us
  Pallas kernels  410 us (100%)
    pallas_call x1, Pallas kernels, block_sums(): pl.pallas_call(functools.partial(body, cfg), name='mlp_sums', out_shape=(...  376 us
    pallas_call x1, Pallas kernels, place(): pl.pallas_call(kernel, name='place', out_shape=jax.ShapeDtypeStruct((n *...  33.7 us

profile of v1, /device:TPU:0, one launch (start us, length us, event | category | flops | bytes accessed | tf_op | source)
XLA Modules:
  0.0 410.0 jit_solution(4756852826031794029)
XLA Ops:
  0.0 376.2 %mlp_sums.1 = (bf16[8,2,2,4,2,256,256]{6,5,4,3,2,1,0:T(8,128)(2,1)}, bf16[8,2,4,4,256,128]{5,4,3,2,1,0:T(8,128)(2,1)}) custom-call(bf16[2048,12288]{1,0:T(8,128)(2,1)} %x_ref.1, bf16[12288,896]{1,0:T(8,128)(2,1)} %wg_ref.1, bf16[12288,896]{1,0:T(8,128)(2,1)} %wu_ref.1, bf16[896,12288]{1,0:T(8,128)(2,1)} %wdh_ref.1), custom_call_target="tpu_custom_call" | custom-call | tf_op jit(solution)/shard_map/mlp_sums/pallas_call | solution.py:715
  376.3 33.7 %place.1 = bf16[2048,12288]{1,0:T(8,128)(2,1)} custom-call(bf16[8,2,2,4,2,256,256]{6,5,4,3,2,1,0:T(8,128)(2,1)} %get-tuple-element.7.a_ref, bf16[8,2,4,4,256,128]{5,4,3,2,1,0:T(8,128)(2,1)} %get-tuple-element.8.b_ref), custom_call_target="tpu_custom_call" | custom-call | tf_op jit(solution)/shard_map/place/pallas_call | solution.py:773

commit v2 on v1

--- a/solution.py
+++ b/solution.py
@@ -17,12 +17,12 @@
     return dict(n=rows // chunk, R=chunk, D=d, FF=ff, WA=wa, H=wa // 2, WB=wa // 4, NK=pieces, KB=d // pieces)
 
 
-def body(cfg, x_ref, wg_ref, wu_ref, wdh_ref, ta, tb, wd, h, xb, wgb, wub, accg, accu, ps, pr, a2s, a2r, a3s, a3r, t1s, t1r, t2s, t2r,
+def body(cfg, x_ref, wg_ref, wu_ref, wdh_ref, ta, tb, wd, h, xb, wb, acc, ps, pr, a2s, a2r, a3s, a3r, t1s, t1r, t2s, t2r,
          b1s, b1r, b2s, b2r, b3s, b3r, b4s, b4r, b5s, b5r, fa, fb,
          wd_m, g_m, p_s, p_m, a2_s, a2_m, a3_s, a3_m, t1_s, t1_m, t2_s, t2_m, b1_s, b1_m, b2_s, b2_m, b3_s, b3_m, b4_s, b4_m, b5_s, b5_m,
          la_m, lb_m, fa_s, fb_s, q_s, g1_m, g2_m, g3_m, g4_m, g5_m, h1_m, h2_m, hz_m, h5_m,
          cp, ca2, ca3, ct1, ct2, cb1, cb2, cb3, cb4, cb5):
-    n, R, D, WA, H, WB, NK, KB = (cfg[k] for k in ("n", "R", "D", "WA", "H", "WB", "NK", "KB"))
+    n, R, D, FF, WA, H, WB, NK, KB = (cfg[k] for k in ("n", "R", "D", "FF", "WA", "H", "WB", "NK", "KB"))
     NB = xb.shape[0]
     me = lax.axis_index("tp")
     dp = lax.axis_index("dp")
@@ -112,8 +112,14 @@
         i, k, b = kk // NK, kk % NK, kk % NB
         rows, ks = pl.ds(pl.multiple_of(i * R, R), R), pl.ds(pl.multiple_of(k * KB, KB), KB)
         return (pltpu.make_async_copy(x_ref.at[rows, ks], xb.at[b], g_m.at[b, 0]),
-                pltpu.make_async_copy(wg_ref.at[ks], wgb.at[b], g_m.at[b, 1]),
-                pltpu.make_async_copy(wu_ref.at[ks], wub.at[b], g_m.at[b, 2]))
+                pltpu.make_async_copy(wg_ref.at[ks], wb.at[b, :, pl.ds(0, FF)], g_m.at[b, 1]),
+                pltpu.make_async_copy(wu_ref.at[ks], wb.at[b, :, pl.ds(FF, FF)], g_m.at[b, 2]))
+
+    def wd_copy(k):
+        core, m = jnp.where(k < 3, 1 - c, c), k % 3
+        off = jnp.where(m < 2, col_a(core, m, 0), col_b(core, 0))
+        cols = pl.ds(pl.multiple_of(off, 4 * WA), 4 * WA)
+        return pltpu.make_async_copy(wdh_ref.at[:, cols], wd.at[:, cols], wd_m.at[k])
 
     def g_pieces(i, k0, k1):
         def step(k, _):
@@ -122,23 +128,26 @@
             for cp_ in g_copies(kk):
                 cp_.wait()
 
-            @pl.when(kk + NB - 1 < n * NK)
+            @pl.when(kk == NK - 1)
+            def _():
+                for p in range(6):
+                    wd_copy(p).start()
+
+            @pl.when((kk + NB - 1 < n * NK))
             def _():
                 for cp_ in g_copies(kk + NB - 1):
                     cp_.start()
 
             @pl.when(k == 0)
             def _():
-                accg[...] = jnp.zeros_like(accg)
-                accu[...] = jnp.zeros_like(accu)
-
-            accg[...] += jnp.dot(xb[b], wgb[b], preferred_element_type=F32)
-            accu[...] += jnp.dot(xb[b], wub[b], preferred_element_type=F32)
+                acc[...] = jnp.zeros_like(acc)
+
+            acc[...] += jnp.dot(xb[b], wb[b], preferred_element_type=F32)
             return 0
 
         lax.fori_loop(k0, k1, step, 0)
         if k1 == NK:
-            h[i % 3] = (jax.nn.silu(accg[...]) * accu[...]).astype(BF16)
+            h[i % 3] = (jax.nn.silu(acc[:, :FF]) * acc[:, FF:]).astype(BF16)
 
     def s1(t):
         @pl.when(t >= 1)
@@ -150,6 +159,10 @@
             pl.semaphore_wait(cp, 1)
 
         def step(j, _):
+            @pl.when((t == 0) & (j % 4 == 0))
+            def _():
+                wd_copy(j // 4).wait()
+
             col = jnp.where(j < 8, col_a(1 - c, 0, j), col_b(1 - c, j - 8))
             ps[j] = dot(t, col, WA, WA).astype(BF16)
             copy(ps.at[j], pr.at[t % 2, j], p_s, p_m.at[t % 2], partner).start()
@@ -196,6 +209,11 @@
         lax.fori_loop(0, 2, step, 0)
 
     def t1(t):
+        @pl.when(t == 0)
+        def _():
+            for p in range(3, 6):
+                wd_copy(p).wait()
+
         c_p(t % 2).wait_recv()
 
         @pl.when(outer)
@@ -581,26 +599,11 @@
         for cp_ in g_copies(kk):
             cp_.start()
 
-    def wd_copies():
-        out = []
-        for k, core in enumerate((1 - c, c)):
-            for m, (off, w) in enumerate(((col_a(core, 0, 0), 8 * WA), (col_b(core, 0), 16 * WB))):
-                cols = pl.ds(pl.multiple_of(off, w), w)
-                out.append(pltpu.make_async_copy(wdh_ref.at[:, cols], wd.at[:, cols], wd_m.at[2 * k + m]))
-        return out
-
-    g_pieces(0, 0, NK // 2)
-    for cp_ in wd_copies():
-        cp_.start()
-    g_pieces(0, NK // 2, NK)
+    g_pieces(0, 0, NK)
+    s1(0)
     cut = [NK * k // 8 for k in range(9)]
 
     def slot(t, _):
-        @pl.when(t == 0)
-        def _():
-            for cp_ in wd_copies():
-                cp_.wait()
-
         def at(i, f):
             @pl.when((i >= 0) & (i < n))
             def _():
@@ -610,40 +613,39 @@
             at(t + 1, lambda i: g_pieces(i, cut[a], cut[b]))
 
         u, v, w, e = t - 1, t - 2, t - 3, t - 4
-        at(u, t3)
-        at(t, s1)
-        at(w, q2b)
         at(v, q0a)
+        at(t - 8, q4b)
         at(u, s4)
         g(0, 1)
         at(t, t1)
-        at(v, q0b)
         at(u, t4)
         at(t, lambda i: s2(i, 0))
+        at(u, s5)
+        at(v, q1b)
+        at(t - 7, q4a)
         g(1, 2)
+        at(u, t5)
+        at(t - 7, q3a)
+        at(t, lambda i: s2(i, 1))
+        g(2, 3)
         at(e, q2a)
-        at(u, s5)
-        at(w, q3a)
-        at(w, q3b)
-        g(2, 3)
-        at(u, t5)
+        at(e, q3b)
         g(3, 4)
-        at(t, lambda i: s2(i, 1))
         at(t, t2)
-        at(v, q1b)
-        g(4, 5)
-        at(t, s3)
-        g(5, 7)
+        g(4, 6)
         at(u, s6)
         at(u, t6)
-        at(e, q4a)
-        at(e, q5)
+        at(t, s3)
+        g(6, 8)
         at(v, q1a)
-        g(7, 8)
-        at(e, q4b)
+        at(t - 8, q5)
+        at(t, t3)
+        at(v, q2b)
+        at(t + 1, s1)
+        at(u, q0b)
         return 0
 
-    lax.fori_loop(0, n + 4, slot, 0)
+    lax.fori_loop(0, n + 8, slot, 0)
 
     last = n - 1
     c_p(0).wait_send()
@@ -696,17 +698,17 @@
 
 def block_sums(cfg, x, w_gate, w_up, w_down):
     n, R, D, FF, WA, H, WB, KB = (cfg[k] for k in ("n", "R", "D", "FF", "WA", "H", "WB", "KB"))
-    NB = 4
+    NB = 3
     vm = lambda *s: pltpu.VMEM(s, BF16)
     dma = lambda *s: pltpu.SemaphoreType.DMA(s) if s else pltpu.SemaphoreType.DMA
     reg = lambda *s: pltpu.SemaphoreType.REGULAR(s) if s else pltpu.SemaphoreType.REGULAR
     scratch = [
-        vm(FF, D), vm(3, R, FF), vm(NB, R, KB), vm(NB, KB, FF), vm(NB, KB, FF), pltpu.VMEM((R, FF), F32), pltpu.VMEM((R, FF), F32),
+        vm(FF, D), vm(3, R, FF), vm(NB, R, KB), vm(NB, KB, 2 * FF), pltpu.VMEM((R, 2 * FF), F32),
         vm(12, R, WA), vm(2, 12, R, WA), vm(2, 2, R, WA), vm(2, 2, 2, R, WA), vm(2, R, WA), vm(2, 2, R, WA),
         vm(2, R, H), vm(2, R, H), vm(2, R, H), vm(2, 2, R, H),
         vm(R, WA), vm(R, WA), vm(R, WA), vm(2, R, WA), vm(2, R, WA), vm(2, R, WA), vm(2, R, WB), vm(2, R, WB), vm(R, WB), vm(R, WB),
         vm(2, R, H), vm(R, WB),
-        dma(4), dma(NB, 3), dma(), dma(2), dma(2, 2), dma(2, 2, 2), dma(2), dma(2, 2), dma(2), dma(2), dma(2), dma(2, 2),
+        dma(6), dma(NB, 3), dma(), dma(2), dma(2, 2), dma(2, 2, 2), dma(2), dma(2, 2), dma(2), dma(2), dma(2), dma(2, 2),
         dma(), dma(), dma(), dma(2), dma(2), dma(2), dma(2), dma(2), dma(), dma(),
         dma(2), dma(), dma(2, 5), dma(2), dma(N_OPS), dma(n), dma(n), dma(2, n), dma(4, n), dma(n), dma(n), dma(2, n), dma(6, n), dma(n),
         reg(), reg(2), reg(2), reg(), reg(), reg(), reg(), reg(2), reg(), reg(),
@@ -725,7 +727,7 @@
 
 def place(cfg, ta, tb):
     n, R, D, WA, H, WB = (cfg[k] for k in ("n", "R", "D", "WA", "H", "WB"))
-    W, NBUF = 8 * WA, 4
+    W, NBUF, AHEAD = 8 * WA, 8, 4
 
     def kernel(a_ref, b_ref, o_ref, buf, in_m, out_m):
         def ins(i, part, b):
@@ -748,17 +750,17 @@
                     for cp in ins(s // 3, part, b):
                         cp.start()
 
-        for s in range(2):
+        for s in range(AHEAD):
             start(s)
 
         def step(s, _):
-            @pl.when(s >= 2)
-            def _():
-                out(s - 2, (s - 2) % NBUF).wait()
-
-            @pl.when(s + 2 < 3 * n)
-            def _():
-                start(s + 2)
+            @pl.when(s >= NBUF - AHEAD)
+            def _():
+                out(s - NBUF + AHEAD, (s + AHEAD) % NBUF).wait()
+
+            @pl.when(s + AHEAD < 3 * n)
+            def _():
+                start(s + AHEAD)
 
             b = s % NBUF
             pltpu.make_async_copy(buf.at[b], buf.at[b], in_m.at[b]).wait()
@@ -766,7 +768,7 @@
             return 0
 
         lax.fori_loop(0, 3 * n, step, 0)
-        for s in (3 * n - 2, 3 * n - 1):
+        for s in range(3 * n - NBUF + AHEAD, 3 * n):
             out(s, s % NBUF).wait()
 
     hbm = pl.BlockSpec(memory_space=pl.ANY)
@@ -795,4 +797,4 @@
 
 
 def solution(mesh):
-    return build(mesh, 256, 16)
+    return build(mesh, 256, 12)

time: 410 us -> 400 us (0.976)
  Pallas kernels: 410 us -> 398 us
    pallas_call x1, Pallas kernels: 376 us -> 365 us  [block_sums(): pl.pallas_call(functools.partial(body, cfg), name='mlp_sums', out_shape=(...]
where the time goes in v2:
time: 400 us; the launch traced here: 398 us
  Pallas kernels  398 us (100%)
    pallas_call x1, Pallas kernels, block_sums(): pl.pallas_call(functools.partial(body, cfg), name='mlp_sums', out_shape=(...  365 us
    pallas_call x1, Pallas kernels, place(): pl.pallas_call(kernel, name='place', out_shape=jax.ShapeDtypeStruct((n *...  33.7 us

profile of v2, /device:TPU:0, one launch (start us, length us, event | category | flops | bytes accessed | tf_op | source)
XLA Modules:
  0.0 398.4 jit_solution(860027788305932428)
XLA Ops:
  0.0 364.7 %mlp_sums.1 = (bf16[8,2,2,4,2,256,256]{6,5,4,3,2,1,0:T(8,128)(2,1)}, bf16[8,2,4,4,256,128]{5,4,3,2,1,0:T(8,128)(2,1)}) custom-call(bf16[2048,12288]{1,0:T(8,128)(2,1)} %x_ref.1, bf16[12288,896]{1,0:T(8,128)(2,1)} %wg_ref.1, bf16[12288,896]{1,0:T(8,128)(2,1)} %wu_ref.1, bf16[896,12288]{1,0:T(8,128)(2,1)} %wdh_ref.1), custom_call_target="tpu_custom_call" | custom-call | tf_op jit(solution)/shard_map/mlp_sums/pallas_call | solution.py:717
  364.7 33.7 %place.1 = bf16[2048,12288]{1,0:T(8,128)(2,1)} custom-call(bf16[8,2,2,4,2,256,256]{6,5,4,3,2,1,0:T(8,128)(2,1)} %get-tuple-element.7.a_ref, bf16[8,2,4,4,256,128]{5,4,3,2,1,0:T(8,128)(2,1)} %get-tuple-element.8.b_ref), custom_call_target="tpu_custom_call" | custom-call | tf_op jit(solution)/shard_map/place/pallas_call | solution.py:775

commit v3 on v2

--- a/solution.py
+++ b/solution.py
@@ -1,4 +1,5 @@
 import functools
+import math
 
 import jax
 import jax.numpy as jnp
@@ -17,13 +18,18 @@
     return dict(n=rows // chunk, R=chunk, D=d, FF=ff, WA=wa, H=wa // 2, WB=wa // 4, NK=pieces, KB=d // pieces)
 
 
-def body(cfg, x_ref, wg_ref, wu_ref, wdh_ref, ta, tb, wd, h, xb, wb, acc, ps, pr, a2s, a2r, a3s, a3r, t1s, t1r, t2s, t2r,
+def staged(cfg):
+    return min((cfg["FF"] + cfg["KB"]) // cfg["R"], cfg["n"] - 1)
+
+
+def body(cfg, x_ref, wg_ref, wu_ref, wdh_ref, tot, big, h, xb, acc, a2s, a2r, a3s, a3r, t1s, t1r, t2s, t2r,
          b1s, b1r, b2s, b2r, b3s, b3r, b4s, b4r, b5s, b5r, fa, fb,
-         wd_m, g_m, p_s, p_m, a2_s, a2_m, a3_s, a3_m, t1_s, t1_m, t2_s, t2_m, b1_s, b1_m, b2_s, b2_m, b3_s, b3_m, b4_s, b4_m, b5_s, b5_m,
+         wd_m, g_m, st_m, p_s, p_m, a2_s, a2_m, a3_s, a3_m, t1_s, t1_m, t2_s, t2_m, b1_s, b1_m, b2_s, b2_m, b3_s, b3_m, b4_s, b4_m, b5_s, b5_m,
          la_m, lb_m, fa_s, fb_s, q_s, g1_m, g2_m, g3_m, g4_m, g5_m, h1_m, h2_m, hz_m, h5_m,
          cp, ca2, ca3, ct1, ct2, cb1, cb2, cb3, cb4, cb5):
     n, R, D, FF, WA, H, WB, NK, KB = (cfg[k] for k in ("n", "R", "D", "FF", "WA", "H", "WB", "NK", "KB"))
     NB = xb.shape[0]
+    S = staged(cfg)
     me = lax.axis_index("tp")
     dp = lax.axis_index("dp")
     x, y, z, c = me // 16, (me // 8) % 2, (me // 2) % 4, me % 2
@@ -76,10 +82,25 @@
         return pl.ds(pl.multiple_of(i * w, w), w)
 
     def dot(i, col, w, unit):
-        return jnp.dot(h[i % 3], wd[:, pl.ds(pl.multiple_of(col, unit), w)], preferred_element_type=F32)
+        return jnp.dot(h[i % 3], big[pl.ds(0, FF), pl.ds(pl.multiple_of(col, unit), w)], preferred_element_type=F32)
+
+    def weights(b, off, w):
+        return pl.ds(FF, KB), pl.ds(pl.multiple_of(b * 2 * FF + off, FF), w)
+
+    def tile(k, off=0, w=WA):
+        across, first = (D - NB * 2 * FF) // WA, NB * 2 * FF
+        row, col = FF + k // across * R, first + k % across * WA + off
+        return (pl.ds(pl.multiple_of(row, math.gcd(FF, R)), R), pl.ds(pl.multiple_of(col, math.gcd(first, WB)), w))
+
+    def p_in(s, j, off=0, w=WA):
+        return big[tile(s * 12 + j, off, w)].astype(F32)
+
+    def p_tile(k):
+        return big.at[tile(k)]
 
     def c_p(s):
-        return copy(ps, pr.at[s], p_s, p_m.at[s], partner)
+        every = big.at[pl.ds(0, R), pl.ds(0, 12 * WA)]
+        return copy(every, every, p_s, p_m.at[s], partner)
 
     def c_a2(s, o, m):
         return copy(a2s.at[o, m], a2r.at[s, o, m], a2_s.at[o, m], a2_m.at[s, o, m], fn(o))
@@ -112,14 +133,14 @@
         i, k, b = kk // NK, kk % NK, kk % NB
         rows, ks = pl.ds(pl.multiple_of(i * R, R), R), pl.ds(pl.multiple_of(k * KB, KB), KB)
         return (pltpu.make_async_copy(x_ref.at[rows, ks], xb.at[b], g_m.at[b, 0]),
-                pltpu.make_async_copy(wg_ref.at[ks], wb.at[b, :, pl.ds(0, FF)], g_m.at[b, 1]),
-                pltpu.make_async_copy(wu_ref.at[ks], wb.at[b, :, pl.ds(FF, FF)], g_m.at[b, 2]))
+                pltpu.make_async_copy(wg_ref.at[ks], big.at[weights(b, 0, FF)], g_m.at[b, 1]),
+                pltpu.make_async_copy(wu_ref.at[ks], big.at[weights(b, FF, FF)], g_m.at[b, 2]))
 
     def wd_copy(k):
         core, m = jnp.where(k < 3, 1 - c, c), k % 3
         off = jnp.where(m < 2, col_a(core, m, 0), col_b(core, 0))
         cols = pl.ds(pl.multiple_of(off, 4 * WA), 4 * WA)
-        return pltpu.make_async_copy(wdh_ref.at[:, cols], wd.at[:, cols], wd_m.at[k])
+        return pltpu.make_async_copy(wdh_ref.at[:, cols], big.at[pl.ds(0, FF), cols], wd_m.at[k])
 
     def g_pieces(i, k0, k1):
         def step(k, _):
@@ -142,7 +163,7 @@
             def _():
                 acc[...] = jnp.zeros_like(acc)
 
-            acc[...] += jnp.dot(xb[b], wb[b], preferred_element_type=F32)
+            acc[...] += jnp.dot(xb[b], big[weights(b, 0, 2 * FF)], preferred_element_type=F32)
             return 0
 
         lax.fori_loop(k0, k1, step, 0)
@@ -164,8 +185,8 @@
                 wd_copy(j // 4).wait()
 
             col = jnp.where(j < 8, col_a(1 - c, 0, j), col_b(1 - c, j - 8))
-            ps[j] = dot(t, col, WA, WA).astype(BF16)
-            copy(ps.at[j], pr.at[t % 2, j], p_s, p_m.at[t % 2], partner).start()
+            p_tile(24 + j)[...] = dot(t, col, WA, WA).astype(BF16)
+            copy(p_tile(24 + j), p_tile(t % 2 * 12 + j), p_s, p_m.at[t % 2], partner).start()
             return 0
 
         lax.fori_loop(0, 12, step, 0)
@@ -182,7 +203,7 @@
                     pl.semaphore_wait(ca2.at[o], 1)
 
             g = gf(o) if m else gd
-            v = dot(t, col_a(c, o, g), WA, WA) + pr[t % 2, o * 4 + g].astype(F32)
+            v = dot(t, col_a(c, o, g), WA, WA) + p_in(t % 2, o * 4 + g)
             a2s[o, m] = v.astype(BF16)
             c_a2(t % 2, o, m).start()
             return 0
@@ -201,7 +222,7 @@
 
             c_a2(t % 2, o, 0).wait_recv()
             g = gs(o)
-            v = dot(t, col_a(c, o, g), WA, WA) + pr[t % 2, o * 4 + g].astype(F32) + a2r[t % 2, o, 0].astype(F32)
+            v = dot(t, col_a(c, o, g), WA, WA) + p_in(t % 2, o * 4 + g) + a2r[t % 2, o, 0].astype(F32)
             a3s[o] = v.astype(BF16)
             c_a3(t % 2, o).start()
             return 0
@@ -224,7 +245,7 @@
                 pl.semaphore_wait(cb1, 1)
 
             q = 3 - z
-            b1s[...] = (dot(t, col_b(c, q), WA, WA) + pr[t % 2, 8 + q].astype(F32)).astype(BF16)
+            b1s[...] = (dot(t, col_b(c, q), WA, WA) + p_in(t % 2, 8 + q)).astype(BF16)
             c_b1().start()
 
     def t2(t):
@@ -238,7 +259,7 @@
             c_b1().wait_recv()
 
         q = (z + 2) % 4
-        b2s[...] = (dot(t, col_b(c, q), WA, WA) + pr[t % 2, 8 + q].astype(F32) + b1r[...].astype(F32)).astype(BF16)
+        b2s[...] = (dot(t, col_b(c, q), WA, WA) + p_in(t % 2, 8 + q) + b1r[...].astype(F32)).astype(BF16)
         d = jnp.where(z < 2, 0, 1)
         c_b2(d).start()
 
@@ -270,7 +291,7 @@
 
     def own_a(u, o, half):
         s, ln = u % 2, lanes(half, H)
-        return (dot(u, col_a(c, o, go, half), H, H) + pr[s, o * 4 + go, :, ln].astype(F32)
+        return (dot(u, col_a(c, o, go, half), H, H) + p_in(s, o * 4 + go, half * H, H)
                 + a2r[s, o, 1, :, ln].astype(F32) + a3r[s, o, :, ln].astype(F32))
 
     def s5(u):
@@ -300,8 +321,14 @@
         def _():
             signal(ct1, zout_d)
 
+    def rows(v):
+        return pl.ds(pl.multiple_of(v * R, R), R)
+
     def win_a(u, o, g, half):
-        return ta.at[u, c, o, g, half]
+        return tot.at[rows(u), pl.ds(pl.multiple_of(col_a(c, o, g, half), H), H)]
+
+    def win_b(u, q, g=0, w=WB):
+        return tot.at[rows(u), pl.ds(pl.multiple_of(col_b(c, q, g), WB), w)]
 
     def fa_copies(u, o):
         w = win_a(u, o, go, near)
@@ -364,7 +391,7 @@
                     c_b2(d).wait_recv()
 
                 q = pick(d, zu, zd)
-                b3s[d] = (dot(u, col_b(c, q), WA, WA) + pr[u % 2, 8 + q].astype(F32) + b2r[d].astype(F32)).astype(BF16)
+                b3s[d] = (dot(u, col_b(c, q), WA, WA) + p_in(u % 2, 8 + q) + b2r[d].astype(F32)).astype(BF16)
                 c_b3(d, to).start()
 
             return 0
@@ -378,7 +405,7 @@
 
     def own_b(u, g):
         ln = lanes(g, WB)
-        return (dot(u, col_b(c, z, g), WB, WB) + pr[u % 2, 8 + z, :, ln].astype(F32)
+        return (dot(u, col_b(c, z, g), WB, WB) + p_in(u % 2, 8 + z, g * WB, WB)
                 + b3r[0, :, ln].astype(F32) + b3r[1, :, ln].astype(F32))
 
     def t4(u):
@@ -420,11 +447,11 @@
         c_b5(o).start()
 
     def fb_copies(u):
-        w, o = tb.at[u, c, z, go], u % 2
+        w, o = win_b(u, z, go), u % 2
         return ((fb, w, fb_s.at[0], h1_m.at[u], sn(o)), (fb, w, fb_s.at[1], h2_m.at[0, u], fn(o)))
 
     def fb_local(u):
-        return pltpu.make_async_copy(fb, tb.at[u, c, z, go], lb_m)
+        return pltpu.make_async_copy(fb, win_b(u, z, go), lb_m)
 
     def t6(u):
         o = u % 2
@@ -496,8 +523,8 @@
         for half in range(2):
             op("q4", True, functools.partial(lambda o, half, v: win_a(v, o, gf(o), half), o, half), lambda v: g5_m.at[v], partner)
             op("q5", True, functools.partial(lambda o, half, v: win_a(v, o, gd, half), o, half), lambda v: g5_m.at[v], partner)
-    op("r0", True, lambda v: tb.at[v, c, z, gs(v % 2)], lambda v: h2_m.at[1, v], None)
-    block = lambda q: (lambda v: tb.at[v, c, q])
+    op("r0", True, lambda v: win_b(v, z, gs(v % 2)), lambda v: h2_m.at[1, v], None)
+    block = lambda q: (lambda v: win_b(v, q, w=4 * WB))
     op("r1", up_ok, block(z), lambda v: hz_m.at[0, v], up)
     op("r1", dn_ok, block(z), lambda v: hz_m.at[1, v], down)
     op("r1", True, block(z), lambda v: h5_m.at[v], partner)
@@ -521,7 +548,7 @@
         copy(ref, ref, q_s.at[0], sem, partner).wait_recv()
 
     def pair(v):
-        return ta.at[v, c, :, 0, 0]
+        return tot.at[rows(v), pl.ds(0, WA)]
 
     def q0a(v):
         arrived(pair(v), g1_m.at[v])
@@ -530,7 +557,7 @@
         run("q0o", v)
 
     def q0b(v):
-        arrived(tb.at[v, c, 0, 0], h1_m.at[v])
+        arrived(win_b(v, 0), h1_m.at[v])
         run("r0", v)
 
     def q1a(v):
@@ -543,7 +570,7 @@
     def q1b(v):
         fb_local(v).wait()
         for k in range(2):
-            arrived(tb.at[v, c, 0, 0], h2_m.at[k, v])
+            arrived(win_b(v, 0), h2_m.at[k, v])
         run("r1", v)
 
     def q2a(v):
@@ -558,7 +585,7 @@
         for there, kk, g in ((up_there, k, groups[0]), (down_there, k + 1, groups[1])):
             @pl.when(there)
             def _():
-                arrived(tb.at[v, c, 0], hz_m.at[kk, v])
+                arrived(win_b(v, 0, w=4 * WB), hz_m.at[kk, v])
 
             run(g, v)
 
@@ -580,6 +607,14 @@
         for k in range(2):
             arrived(pair(v), g4_m.at[2 + k, v])
         run("q5", v)
+
+    def all_here(v):
+        arrived(tot.at[rows(v), pl.ds(0, 8 * WA)], g5_m.at[v])
+        arrived(tot.at[rows(v), pl.ds(0, 16 * WB)], h5_m.at[v])
+
+    def stage(v):
+        all_here(v)
+        pltpu.make_async_copy(tot.at[rows(v)], big.at[rows(v)], st_m.at[v]).start()
 
     @pl.when(outer)
     def _():
@@ -643,12 +678,15 @@
         at(v, q2b)
         at(t + 1, s1)
         at(u, q0b)
+        pl.when(t == n + 1)(lambda: c_p(0).wait_send())
+
+        pl.when((t > n) & (t <= n + S))(lambda: stage(t - n - 1))
+
         return 0
 
     lax.fori_loop(0, n + 8, slot, 0)
 
     last = n - 1
-    c_p(0).wait_send()
     for o in range(2):
         for m in range(2):
             c_a2(0, o, m).wait_send()
@@ -685,12 +723,10 @@
         else:
             pl.when(cond)(done)
 
-    def all_here(v, _):
-        arrived(ta.at[v, 1 - c], g5_m.at[v])
-        arrived(tb.at[v, 1 - c], h5_m.at[v])
-        return 0
-
-    lax.fori_loop(0, n, all_here, 0)
+    for v in range(S, n):
+        all_here(v)
+    for v in range(S):
+        pltpu.make_async_copy(tot.at[rows(v)], big.at[rows(v)], st_m.at[v]).wait()
 
 
 N_OPS = 2 + 6 * 3 + 8 + 8 + 1 + 3 + 8 + 1
@@ -703,12 +739,12 @@
     dma = lambda *s: pltpu.SemaphoreType.DMA(s) if s else pltpu.SemaphoreType.DMA
     reg = lambda *s: pltpu.SemaphoreType.REGULAR(s) if s else pltpu.SemaphoreType.REGULAR
     scratch = [
-        vm(FF, D), vm(3, R, FF), vm(NB, R, KB), vm(NB, KB, 2 * FF), pltpu.VMEM((R, 2 * FF), F32),
-        vm(12, R, WA), vm(2, 12, R, WA), vm(2, 2, R, WA), vm(2, 2, 2, R, WA), vm(2, R, WA), vm(2, 2, R, WA),
+        vm(3, R, FF), vm(NB, R, KB), pltpu.VMEM((R, 2 * FF), F32),
+        vm(2, 2, R, WA), vm(2, 2, 2, R, WA), vm(2, R, WA), vm(2, 2, R, WA),
         vm(2, R, H), vm(2, R, H), vm(2, R, H), vm(2, 2, R, H),
         vm(R, WA), vm(R, WA), vm(R, WA), vm(2, R, WA), vm(2, R, WA), vm(2, R, WA), vm(2, R, WB), vm(2, R, WB), vm(R, WB), vm(R, WB),
         vm(2, R, H), vm(R, WB),
-        dma(6), dma(NB, 3), dma(), dma(2), dma(2, 2), dma(2, 2, 2), dma(2), dma(2, 2), dma(2), dma(2), dma(2), dma(2, 2),
+        dma(6), dma(NB, 3), dma(staged(cfg)), dma(), dma(2), dma(2, 2), dma(2, 2, 2), dma(2), dma(2, 2), dma(2), dma(2), dma(2), dma(2, 2),
         dma(), dma(), dma(), dma(2), dma(2), dma(2), dma(2), dma(2), dma(), dma(),
         dma(2), dma(), dma(2, 5), dma(2), dma(N_OPS), dma(n), dma(n), dma(2, n), dma(4, n), dma(n), dma(n), dma(2, n), dma(6, n), dma(n),
         reg(), reg(2), reg(2), reg(), reg(), reg(), reg(), reg(2), reg(), reg(),
@@ -717,69 +753,53 @@
     return pl.pallas_call(
         functools.partial(body, cfg),
         name="mlp_sums",
-        out_shape=(jax.ShapeDtypeStruct((n, 2, 2, 4, 2, R, H), BF16), jax.ShapeDtypeStruct((n, 2, 4, 4, R, WB), BF16)),
+        out_shape=(jax.ShapeDtypeStruct((n * R, D), BF16), vm(FF + KB, D)),
         in_specs=[hbm] * 4,
-        out_specs=(hbm, hbm),
+        out_specs=(hbm, pl.BlockSpec(memory_space=pltpu.VMEM)),
         scratch_shapes=scratch,
-        compiler_params=pltpu.CompilerParams(has_side_effects=True, vmem_limit_bytes=66_000_000),
+        compiler_params=pltpu.CompilerParams(has_side_effects=True, vmem_limit_bytes=18_000_000),
     )(x, w_gate, w_up, w_down)
 
 
-def place(cfg, ta, tb):
-    n, R, D, WA, H, WB = (cfg[k] for k in ("n", "R", "D", "WA", "H", "WB"))
-    W, NBUF, AHEAD = 8 * WA, 8, 4
-
-    def kernel(a_ref, b_ref, o_ref, buf, in_m, out_m):
-        def ins(i, part, b):
-            if part < 2:
-                return [pltpu.make_async_copy(a_ref.at[i, part, o, g, k], buf.at[b, :, pl.ds((o * 4 + g) * WA + k * H, H)], in_m.at[b])
-                        for o in range(2) for g in range(4) for k in range(2)]
-            return [pltpu.make_async_copy(b_ref.at[i, c, q, g], buf.at[b, :, pl.ds(((c * 4 + q) * 4 + g) * WB, WB)], in_m.at[b])
-                    for c in range(2) for q in range(4) for g in range(4)]
-
-        def out(s, b):
-            i, part = s // 3, s % 3
-            rows = pl.ds(pl.multiple_of(i * R, R), R)
-            return pltpu.make_async_copy(buf.at[b], o_ref.at[rows, pl.ds(pl.multiple_of(part * W, W), W)], out_m.at[b])
-
-        def start(s):
-            b = s % NBUF
-            for part in range(3):
-                @pl.when(s % 3 == part)
-                def _():
-                    for cp in ins(s // 3, part, b):
-                        cp.start()
-
-        for s in range(AHEAD):
-            start(s)
-
-        def step(s, _):
-            @pl.when(s >= NBUF - AHEAD)
-            def _():
-                out(s - NBUF + AHEAD, (s + AHEAD) % NBUF).wait()
-
-            @pl.when(s + AHEAD < 3 * n)
-            def _():
-                start(s + AHEAD)
-
-            b = s % NBUF
-            pltpu.make_async_copy(buf.at[b], buf.at[b], in_m.at[b]).wait()
-            out(s, b).start()
-            return 0
-
-        lax.fori_loop(0, 3 * n, step, 0)
-        for s in range(3 * n - NBUF + AHEAD, 3 * n):
-            out(s, s % NBUF).wait()
-
-    hbm = pl.BlockSpec(memory_space=pl.ANY)
+def place(cfg, total, big):
+    n, R, D = (cfg[k] for k in ("n", "R", "D"))
+    S = staged(cfg)
+    K = 4
+
+    def kernel(t_ref, big_ref, o_ref, buf, in_m, out_m, st_m):
+        def whole(v):
+            rows = pl.ds(v * R, R)
+            return pltpu.make_async_copy(big_ref.at[rows], o_ref.at[rows], st_m.at[v])
+
+        def piece(i):
+            return pl.ds(S * R + i * (R // K), R // K)
+
+        last = (n - S) * K
+        ins = [pltpu.make_async_copy(t_ref.at[piece(i)], buf.at[i], in_m.at[i]) for i in range(last)]
+        outs = [pltpu.make_async_copy(buf.at[i], o_ref.at[piece(i)], out_m.at[i]) for i in range(last)]
+        for cp in ins:
+            cp.start()
+        for v in range(S):
+            whole(v).start()
+        for there, back in zip(ins, outs):
+            there.wait()
+            back.start()
+        for cp in outs:
+            cp.wait()
+        for v in range(S):
+            whole(v).wait()
+
+    hbm, dma = pl.BlockSpec(memory_space=pl.ANY), pltpu.SemaphoreType.DMA
+    parts = (n - S) * K
     return pl.pallas_call(
         kernel,
         name="place",
         out_shape=jax.ShapeDtypeStruct((n * R, D), BF16),
-        in_specs=[hbm, hbm],
+        in_specs=[hbm, pl.BlockSpec(memory_space=pltpu.VMEM)],
         out_specs=hbm,
-        scratch_shapes=[pltpu.VMEM((NBUF, R, W), BF16), pltpu.SemaphoreType.DMA((NBUF,)), pltpu.SemaphoreType.DMA((NBUF,))],
-    )(ta, tb)
+        scratch_shapes=[pltpu.VMEM((parts, R // K, D), BF16), dma((parts,)), dma((parts,)), dma((S,))],
+        compiler_params=pltpu.CompilerParams(vmem_limit_bytes=14_000_000),
+    )(total, pltpu.with_memory_space_constraint(big, pltpu.VMEM))
 
 
 def build(mesh, chunk, pieces):

time: 400 us -> 386 us (0.965)
  Pallas kernels: 398 us -> 384 us
    pallas_call x1, Pallas kernels: 33.7 us -> 17.8 us  [place(): pl.pallas_call(kernel, name='place', out_shape=jax.ShapeDtypeStruct((n *...]
where the time goes in v3:
time: 386 us; the launch traced here: 384 us
  Pallas kernels  384 us (99%)
    pallas_call x1, Pallas kernels, block_sums(): pl.pallas_call(functools.partial(body, cfg), name='mlp_sums', out_shape=(...  366 us
    pallas_call x1, Pallas kernels, place(): pl.pallas_call(kernel, name='place', out_shape=jax.ShapeDtypeStruct((n *...  17.8 us

profile of v3, /device:TPU:0, one launch (start us, length us, event | category | flops | bytes accessed | tf_op | source)
XLA Modules:
  0.0 383.7 jit_solution(3354266631828791147)
XLA Ops:
  0.0 366.0 %mlp_sums.1 = (bf16[2048,12288]{1,0:T(8,128)(2,1)}, bf16[1920,12288]{1,0:T(8,128)(2,1)S(1)}) custom-call(bf16[2048,12288]{1,0:T(8,128)(2,1)} %x_ref.1, bf16[12288,896]{1,0:T(8,128)(2,1)} %wg_ref.1, bf16[12288,896]{1,0:T(8,128)(2,1)} %wu_ref.1, bf16[896,12288]{1,0:T(8,128)(2,1)} %wdh_ref.1), custom_call_target="tpu_custom_call" | custom-call | tf_op jit(solution)/shard_map/mlp_sums/pallas_call | solution.py:753
  366.0 17.8 %place.1 = bf16[2048,12288]{1,0:T(8,128)(2,1)} custom-call(bf16[2048,12288]{1,0:T(8,128)(2,1)} %get-tuple-element.7.t_ref, bf16[1920,12288]{1,0:T(8,128)(2,1)S(1)} %get-tuple-element.8.big_ref), custom_call_target="tpu_custom_call" | custom-call | tf_op jit(solution)/shard_map/place/pallas_call | solution.py:794

commit v4 on v3

--- a/solution.py
+++ b/solution.py
@@ -180,16 +180,18 @@
             pl.semaphore_wait(cp, 1)
 
         def step(j, _):
-            @pl.when((t == 0) & (j % 4 == 0))
-            def _():
-                wd_copy(j // 4).wait()
-
-            col = jnp.where(j < 8, col_a(1 - c, 0, j), col_b(1 - c, j - 8))
-            p_tile(24 + j)[...] = dot(t, col, WA, WA).astype(BF16)
-            copy(p_tile(24 + j), p_tile(t % 2 * 12 + j), p_s, p_m.at[t % 2], partner).start()
+            @pl.when((t == 0) & (j % 2 == 0))
+            def _():
+                wd_copy(j // 2).wait()
+
+            v = dot(t, jnp.where(j < 4, col_a(1 - c, 0, 2 * j), col_b(1 - c, 2 * j - 8)), 2 * WA, WA).astype(BF16)
+            for k in range(2):
+                m = j * 2 + k
+                p_tile(24 + m)[...] = v[:, k * WA:(k + 1) * WA]
+                copy(p_tile(24 + m), p_tile(t % 2 * 12 + m), p_s, p_m.at[t % 2], partner).start()
             return 0
 
-        lax.fori_loop(0, 12, step, 0)
+        lax.fori_loop(0, 6, step, 0)
 
     def s2(t, m):
         def step(o, _):

time: 386 us -> 384 us (level)
  no operation moved by 1% of the time
where the time goes in v4:
time: 384 us; the launch traced here: 382 us
  Pallas kernels  382 us (99%)
    pallas_call x1, Pallas kernels, block_sums(): pl.pallas_call(functools.partial(body, cfg), name='mlp_sums', out_shape=(...  364 us
    pallas_call x1, Pallas kernels, place(): pl.pallas_call(kernel, name='place', out_shape=jax.ShapeDtypeStruct((n *...  17.8 us

profile of v4, /device:TPU:0, one launch (start us, length us, event | category | flops | bytes accessed | tf_op | source)
XLA Modules:
  0.0 382.1 jit_solution(12295505373972352360)
XLA Ops:
  0.0 364.4 %mlp_sums.1 = (bf16[2048,12288]{1,0:T(8,128)(2,1)}, bf16[1920,12288]{1,0:T(8,128)(2,1)S(1)}) custom-call(bf16[2048,12288]{1,0:T(8,128)(2,1)} %x_ref.1, bf16[12288,896]{1,0:T(8,128)(2,1)} %wg_ref.1, bf16[12288,896]{1,0:T(8,128)(2,1)} %wu_ref.1, bf16[896,12288]{1,0:T(8,128)(2,1)} %wdh_ref.1), custom_call_target="tpu_custom_call" | custom-call | tf_op jit(solution)/shard_map/mlp_sums/pallas_call | solution.py:755
  364.4 17.8 %place.1 = bf16[2048,12288]{1,0:T(8,128)(2,1)} custom-call(bf16[2048,12288]{1,0:T(8,128)(2,1)} %get-tuple-element.7.t_ref, bf16[1920,12288]{1,0:T(8,128)(2,1)S(1)} %get-tuple-element.8.big_ref), custom_call_target="tpu_custom_call" | custom-call | tf_op jit(solution)/shard_map/place/pallas_call | solution.py:796

commit v5 on v4

--- a/solution.py
+++ b/solution.py
@@ -618,6 +618,16 @@
         all_here(v)
         pltpu.make_async_copy(tot.at[rows(v)], big.at[rows(v)], st_m.at[v]).start()
 
+    for kk in range(NB - 1):
+        for cp_ in g_copies(kk):
+            cp_.start()
+
+    barrier = pltpu.get_barrier_semaphore()
+    for to in (partner, xn, yn):
+        signal(barrier, to)
+    pl.when(up_ok)(lambda: signal(barrier, up))
+    pl.when(dn_ok)(lambda: signal(barrier, down))
+
     @pl.when(outer)
     def _():
         t1r[...] = jnp.zeros_like(t1r)
@@ -632,11 +642,8 @@
     def _():
         b3r[1] = jnp.zeros_like(b3r[1])
 
-    for kk in range(NB - 1):
-        for cp_ in g_copies(kk):
-            cp_.start()
-
     g_pieces(0, 0, NK)
+    pl.semaphore_wait(barrier, jnp.where(outer, 4, 5))
     s1(0)
     cut = [NK * k // 8 for k in range(9)]
 
@@ -759,7 +766,7 @@
         in_specs=[hbm] * 4,
         out_specs=(hbm, pl.BlockSpec(memory_space=pltpu.VMEM)),
         scratch_shapes=scratch,
-        compiler_params=pltpu.CompilerParams(has_side_effects=True, vmem_limit_bytes=18_000_000),
+        compiler_params=pltpu.CompilerParams(collective_id=0, has_side_effects=True, vmem_limit_bytes=18_000_000),
     )(x, w_gate, w_up, w_down)
 
 

time: 384 us -> 378 us (0.984)
  Pallas kernels: 382 us -> 376 us
    pallas_call x1, Pallas kernels: 364 us -> 358 us  [block_sums(): pl.pallas_call(functools.partial(body, cfg), name='mlp_sums', out_shape=(...]
where the time goes in v5:
time: 378 us; the launch traced here: 376 us
  Pallas kernels  376 us (99%)
    pallas_call x1, Pallas kernels, block_sums(): pl.pallas_call(functools.partial(body, cfg), name='mlp_sums', out_shape=(...  358 us
    pallas_call x1, Pallas kernels, place(): pl.pallas_call(kernel, name='place', out_shape=jax.ShapeDtypeStruct((n *...  17.8 us

profile of v5, /device:TPU:0, one launch (start us, length us, event | category | flops | bytes accessed | tf_op | source)
XLA Modules:
  0.0 376.0 jit_solution(13165891281806216316)
XLA Ops:
  0.0 358.2 %mlp_sums.1 = (bf16[2048,12288]{1,0:T(8,128)(2,1)}, bf16[1920,12288]{1,0:T(8,128)(2,1)S(1)}) custom-call(bf16[2048,12288]{1,0:T(8,128)(2,1)} %x_ref.1, bf16[12288,896]{1,0:T(8,128)(2,1)} %wg_ref.1, bf16[12288,896]{1,0:T(8,128)(2,1)} %wu_ref.1, bf16[896,12288]{1,0:T(8,128)(2,1)} %wdh_ref.1), custom_call_target="tpu_custom_call" | custom-call | tf_op jit(solution)/shard_map/mlp_sums/pallas_call | solution.py:762
  358.2 17.8 %place.1 = bf16[2048,12288]{1,0:T(8,128)(2,1)} custom-call(bf16[2048,12288]{1,0:T(8,128)(2,1)} %get-tuple-element.7.t_ref, bf16[1920,12288]{1,0:T(8,128)(2,1)S(1)} %get-tuple-element.8.big_ref), custom_call_target="tpu_custom_call" | custom-call | tf_op jit(solution)/shard_map/place/pallas_call | solution.py:803

commit v6 on v5

--- a/solution.py
+++ b/solution.py
@@ -687,13 +687,16 @@
         at(v, q2b)
         at(t + 1, s1)
         at(u, q0b)
-        pl.when(t == n + 1)(lambda: c_p(0).wait_send())
-
-        pl.when((t > n) & (t <= n + S))(lambda: stage(t - n - 1))
-
         return 0
 
-    lax.fori_loop(0, n + 8, slot, 0)
+    lax.fori_loop(0, n + 1, slot, 0)
+    c_p(0).wait_send()
+    stages = {f.__name__: f for f in (q0a, q1a, q1b, q2a, q2b, q3a, q3b, q4a, q4b, q5, stage)}
+    for name in ("q0a7", "stage0", "q4b1", "q3a2", "q3a3", "q4a2", "q1b7", "q4b2", "q3b5", "q4b3", "q2a5", "q3a4",
+            "q2a6", "q51", "q52", "stage1", "q1a7", "q4a3", "q3b6", "q4a4", "q3a5", "q3a6", "q4b4", "q4b5",
+            "q4a5", "q2b7", "q2a7", "q53", "stage2", "q54", "stage3", "q55", "stage4", "q4b6", "q3a7", "q4a6",
+            "q3b7", "q56", "stage5", "q57", "q4b7", "q4a7", "stage6"):
+        stages[name[:-1]](jnp.int32(int(name[-1])))
 
     last = n - 1
     for o in range(2):

time: 378 us -> 377 us (level)
  no operation moved by 1% of the time
where the time goes in v6:
time: 377 us
  Pallas kernels  377 us (100%)
    pallas_call x1, Pallas kernels, block_sums(): pl.pallas_call(functools.partial(body, cfg), name='mlp_sums', out_shape=(...  359 us
    pallas_call x1, Pallas kernels, place(): pl.pallas_call(kernel, name='place', out_shape=jax.ShapeDtypeStruct((n *...  17.8 us

profile of v6, /device:TPU:0, one launch (start us, length us, event | category | flops | bytes accessed | tf_op | source)
XLA Modules:
  0.0 377.1 jit_solution(16870168050209339439)
XLA Ops:
  0.0 359.3 %mlp_sums.1 = (bf16[2048,12288]{1,0:T(8,128)(2,1)}, bf16[1920,12288]{1,0:T(8,128)(2,1)S(1)}) custom-call(bf16[2048,12288]{1,0:T(8,128)(2,1)} %x_ref.1, bf16[12288,896]{1,0:T(8,128)(2,1)} %wg_ref.1, bf16[12288,896]{1,0:T(8,128)(2,1)} %wu_ref.1, bf16[896,12288]{1,0:T(8,128)(2,1)} %wdh_ref.1), custom_call_target="tpu_custom_call" | custom-call | tf_op jit(solution)/shard_map/mlp_sums/pallas_call | solution.py:765
  359.4 17.8 %place.1 = bf16[2048,12288]{1,0:T(8,128)(2,1)} custom-call(bf16[2048,12288]{1,0:T(8,128)(2,1)} %get-tuple-element.7.t_ref, bf16[1920,12288]{1,0:T(8,128)(2,1)S(1)} %get-tuple-element.8.big_ref), custom_call_target="tpu_custom_call" | custom-call | tf_op jit(solution)/shard_map/place/pallas_call | solution.py:806
